TPU v7x, 32 devices: a whole 2x2x4 slice. The times are simulated.
32 devices in a mesh: blk: 16 (over z, y, core), row: 2 (over x).
Axes of the slice: x: 2, y: 2, z: 4, core: 2. Of those that a mesh axis runs over, the one named last changes fastest.
Arguments:
- features: float32 [2048, 256], P(('blk', 'row')), may hold values from -2 to 2, as said below
- probes: float32 [2048, 128], P(('blk', 'row')), may hold values from -6 to 6
- outputscale: float32 [1], replicated, may hold values from 0.05 to 0.2
- noise: float32 [1], replicated, may hold values from 0.5 to 2
- pivots: int32 [256], replicated, may hold values from 0 to 2047, as said below
Outputs:
- product: float32 [2048, 128], P(('blk', 'row'))
- preconditioned: float32 [2048, 128], P(('blk', 'row'))
Inputs may be any that keep to these rules, and one draw needn't show every extreme that they name: `pivots`: 256 distinct point indices. real-valued features.
All inputs are finite; a program needn't handle non-finite values.
Results may differ from a plain program's by a relative error of at most 0.0003.
Values sent between devices are 32-bit elements; how exact they have to be, the bound alone decides.
No kernel may reach another device: no remote copies, remote signals or barrier semaphores. Data moves between devices by JAX's collectives and lax.ppermute only.
A program may use at most 64 MiB of HBM per device.

v0:
```python
import jax
import jax.numpy as jnp
from jax import lax
from jax.sharding import PartitionSpec as P

STRIDE = 4
highest = lax.Precision.HIGHEST
root_five = 2.23606797749979


def shifted(block, axis, distance):
    devices = range(lax.axis_size(axis))
    route = [((i - distance) % len(devices), i) for i in devices]
    return lax.ppermute(block, axis, route)


def kernel_tile(row_feats, row_norms, col_feats, col_norms):
    inner = lax.dot_general(
        row_feats,
        col_feats,
        (((1,), (1,)), ((), ())),
        precision=highest,
        preferred_element_type=jnp.float32,
    )
    squared = jnp.maximum(row_norms[:, None] + col_norms[None, :] - 2.0 * inner, 0.0)
    scaled = root_five * jnp.sqrt(squared)
    return (1.0 + scaled + scaled * scaled / 3.0) * jnp.exp(-scaled)


def transposed_product(kernel_block, row_probes):
    return lax.dot_general(
        kernel_block,
        row_probes,
        (((0,), (0,)), ((), ())),
        precision=highest,
        preferred_element_type=jnp.float32,
    )


def quorum_members(block_count, spacing):
    half_count = block_count // 2
    members = list(range(spacing))
    reached = 0
    while reached < half_count:
        reached = reached + spacing
        members.append(reached % block_count)
    return members


def quorum_pairs(block_count, members):
    pair_list = []
    for offset in range(block_count // 2 + 1):
        chosen = None
        for lower_slot, lower_member in enumerate(members):
            for upper_slot, upper_member in enumerate(members):
                if chosen is None and (upper_member - lower_member) % block_count == offset:
                    chosen = (lower_slot, upper_slot)
        two_sided = offset != 0 and 2 * offset != block_count
        pair_list.append((chosen[0], chosen[1], two_sided))
    return pair_list


def member_sweep(fetched, fetched_norms, upper, lower_group, block_rows):
    local_rows, probe_count = fetched[upper][1].shape
    column_sums = jnp.zeros((block_rows, probe_count), jnp.float32)
    arrived_feats = lax.all_gather(fetched[upper][0], "row", axis=0, tiled=True)
    arrived_probes = lax.all_gather(fetched[upper][1], "row", axis=0, tiled=True)
    arrived_norms = jnp.sum(arrived_feats * arrived_feats, axis=1)
    updated = []
    for position, (lower, two_sided) in enumerate(lower_group):
        kernel_block = kernel_tile(
            fetched[lower][0], fetched_norms[lower], arrived_feats, arrived_norms
        )
        updated.append(
            jnp.dot(
                kernel_block, arrived_probes, precision=highest, preferred_element_type=jnp.float32
            )
        )
        if two_sided:
            current = column_sums
            column_sums = current + transposed_product(kernel_block, fetched[lower][1])
    return (tuple(updated), column_sums)


def per_device(features, probes, outputscale, noise, pivots):
    local_rows, probe_count = probes.shape
    block_count = lax.axis_size("blk")
    piece_count = lax.axis_size("row")
    piece_index = lax.axis_index("row")
    amplitude = outputscale[0]
    nugget = noise[0]
    members = quorum_members(block_count, STRIDE)
    pair_list = quorum_pairs(block_count, members)
    slot_count = len(members)
    block_rows = local_rows * piece_count
    own_norms = jnp.sum(features * features, axis=1)
    forward = [jnp.zeros((local_rows, probe_count), jnp.float32) for member in members]
    backward = [jnp.zeros((block_rows, probe_count), jnp.float32) for member in members]
    fetched = [(features, probes)]
    for member in members[1:]:
        fetched.append(shifted((features, probes), "blk", block_count - member))
    fetched_norms = [jnp.sum(entry[0] * entry[0], axis=1) for entry in fetched]
    for upper in range(slot_count):
        lower_group = [
            (lower, two_sided) for lower, target, two_sided in pair_list if target == upper
        ]
        partials, column_sums = member_sweep(fetched, fetched_norms, upper, lower_group, block_rows)
        for position, (lower, two_sided) in enumerate(lower_group):
            forward[lower] = forward[lower] + partials[position]
        backward[upper] = column_sums
    shared = lax.psum_scatter(jnp.stack(backward), "row", scatter_dimension=1, tiled=True)
    kernel_probes = forward[0] + shared[0]
    for position in range(1, slot_count):
        outgoing = forward[position] + shared[position]
        kernel_probes = kernel_probes + shifted(outgoing, "blk", members[position])
    product = amplitude * kernel_probes + nugget * probes
    flat_index = lax.axis_index("blk") * piece_count + piece_index
    offsets = pivots - flat_index * local_rows
    inside = (offsets >= 0) & (offsets < local_rows)
    picked = jnp.where(inside[:, None], features[jnp.clip(offsets, 0, local_rows - 1)], 0.0)
    pivot_feats = lax.psum(picked, ("blk", "row"))
    pivot_norms = jnp.sum(pivot_feats * pivot_feats, axis=1)
    cross = amplitude * kernel_tile(features, own_norms, pivot_feats, pivot_norms)
    gram_part = lax.dot_general(
        cross,
        cross,
        (((0,), (0,)), ((), ())),
        precision=highest,
        preferred_element_type=jnp.float32,
    )
    projected_part = lax.dot_general(
        cross,
        product,
        (((0,), (0,)), ((), ())),
        precision=highest,
        preferred_element_type=jnp.float32,
    )
    gram_sum, projected = lax.psum((gram_part, projected_part), ("blk", "row"))
    inner_pivots = amplitude * kernel_tile(pivot_feats, pivot_norms, pivot_feats, pivot_norms)
    gram = nugget * inner_pivots + gram_sum
    factor = jnp.linalg.cholesky(gram)
    coefficients = jax.scipy.linalg.cho_solve((factor, True), projected)
    preconditioned = (
        product
        - jnp.dot(cross, coefficients, precision=highest, preferred_element_type=jnp.float32)
    ) / nugget
    return (product, preconditioned)


def solution(mesh):
    in_specs = (P(("blk", "row"), None), P(("blk", "row"), None), P(), P(), P())
    out_specs = (P(("blk", "row"), None), P(("blk", "row"), None))
    return jax.shard_map(
        per_device, mesh=mesh, in_specs=in_specs, out_specs=out_specs, check_vma=False
    )
```

profile of v0, /device:TPU:0, one launch (start us, length us, event | category | flops | bytes accessed | tf_op | source)
XLA Modules:
  0.0 363.2 jit_solution(4064739874456005614)
XLA Ops:
  8.0 5.5 %collective-permute-start = (f32[64,256]{1,0:T(8,128)}, f32[64,256]{1,0:T(8,128)S(1)}, u32[]{:S(2)}, u32[]{:S(2)}) collective-permute-start(f32[64,256]{1,0:T(8,128)} %param.5), channel_id=1, source_target_pairs={{2,0},{4,2},{6,4},{8,6},{10,8},{12,10},{14,12},{16,14},{18,16},{20... | collective-permute-start | bytes 196616 | tf_op jit(solution)/shard_map/ppermute | solution.py:14
  14.4 1.4 collective-permute-start.1
  16.5 1.8 gather_fusion
  20.2 5.1 %all_gather.36 = f32[128,256]{1,0:T(8,128)S(1)} all-gather(f32[64,256]{1,0:T(8,128)S(1)} %copy-done), channel_id=1, replica_groups=mesh['blk'=16,'row'=2] {'row'}, dimensions={0}, use_global_device_ids=true | all-gather | bytes 196608 | tf_op jit(solution)/shard_map/all_gather | solution.py:66
  25.2 4.6 %all_gather.37 = f32[128,128]{1,0:T(8,128)S(1)} all-gather(f32[64,128]{1,0:T(8,128)S(1)} %copy-done.1), channel_id=1, replica_groups=mesh['blk'=16,'row'=2] {'row'}, dimensions={0}, use_global_device_ids=true | all-gather | bytes 98304 | tf_op jit(solution)/shard_map/all_gather | solution.py:67
  32.5 4.6 %all_gather.47 = f32[128,128]{1,0:T(8,128)S(1)} all-gather(f32[64,128]{1,0:T(8,128)S(1)} %collective-permute-done.9), channel_id=1, replica_groups=mesh['blk'=16,'row'=2] {'row'}, dimensions={0}, use_global_device_ids=true | all-gather | bytes 98304 | tf_op jit(solution)/shard_map/all_gather | solution.py:67
  37.1 3.2 collective-permute-start.7
  40.3 4.6 %all_gather.39 = f32[128,128]{1,0:T(8,128)S(1)} all-gather(f32[64,128]{1,0:T(8,128)S(1)} %collective-permute-done.1), channel_id=1, replica_groups=mesh['blk'=16,'row'=2] {'row'}, dimensions={0}, use_global_device_ids=true | all-gather | bytes 98304 | tf_op jit(solution)/shard_map/all_gather | solution.py:67
  44.9 1.4 collective-permute-start.3
  46.3 4.6 %all_gather.43 = f32[128,128]{1,0:T(8,128)S(1)} all-gather(f32[64,128]{1,0:T(8,128)S(1)} %collective-permute-done.5), channel_id=1, replica_groups=mesh['blk'=16,'row'=2] {'row'}, dimensions={0}, use_global_device_ids=true | all-gather | bytes 98304 | tf_op jit(solution)/shard_map/all_gather | solution.py:67
  51.0 4.6 %all_gather.45 = f32[128,128]{1,0:T(8,128)S(1)} all-gather(f32[64,128]{1,0:T(8,128)S(1)} %collective-permute-done.7), channel_id=1, replica_groups=mesh['blk'=16,'row'=2] {'row'}, dimensions={0}, use_global_device_ids=true | all-gather | bytes 98304 | tf_op jit(solution)/shard_map/all_gather | solution.py:67
  55.5 3.0 collective-permute-start.8
  58.5 4.6 %all_gather.41 = f32[128,128]{1,0:T(8,128)S(1)} all-gather(f32[64,128]{1,0:T(8,128)S(1)} %collective-permute-done.3), channel_id=1, replica_groups=mesh['blk'=16,'row'=2] {'row'}, dimensions={0}, use_global_device_ids=true | all-gather | bytes 98304 | tf_op jit(solution)/shard_map/all_gather | solution.py:67
  63.1 4.9 %all_gather.38 = f32[128,256]{1,0:T(8,128)S(1)} all-gather(f32[64,256]{1,0:T(8,128)S(1)} %collective-permute-done), channel_id=1, replica_groups=mesh['blk'=16,'row'=2] {'row'}, dimensions={0}, use_global_device_ids=true | all-gather | bytes 196608 | tf_op jit(solution)/shard_map/all_gather | solution.py:66
  68.4 5.0 %all_gather.40 = f32[128,256]{1,0:T(8,128)S(1)} all-gather(f32[64,256]{1,0:T(8,128)S(1)} %collective-permute-done.2), channel_id=1, replica_groups=mesh['blk'=16,'row'=2] {'row'}, dimensions={0}, use_global_device_ids=true | all-gather | bytes 196608 | tf_op jit(solution)/shard_map/all_gather | solution.py:66
  73.9 5.6 %all_gather.42 = f32[128,256]{1,0:T(8,128)S(1)} all-gather(f32[64,256]{1,0:T(8,128)S(1)} %collective-permute-done.4), channel_id=1, replica_groups=mesh['blk'=16,'row'=2] {'row'}, dimensions={0}, use_global_device_ids=true | all-gather | bytes 196608 | tf_op jit(solution)/shard_map/all_gather | solution.py:66
  79.9 4.9 %all_gather.46 = f32[128,256]{1,0:T(8,128)S(1)} all-gather(f32[64,256]{1,0:T(8,128)S(1)} %collective-permute-done.8), channel_id=1, replica_groups=mesh['blk'=16,'row'=2] {'row'}, dimensions={0}, use_global_device_ids=true | all-gather | bytes 196608 | tf_op jit(solution)/shard_map/all_gather | solution.py:66
  85.2 4.9 %all_gather.44 = f32[128,256]{1,0:T(8,128)S(1)} all-gather(f32[64,256]{1,0:T(8,128)S(1)} %collective-permute-done.6), channel_id=1, replica_groups=mesh['blk'=16,'row'=2] {'row'}, dimensions={0}, use_global_device_ids=true | all-gather | bytes 196608 | tf_op jit(solution)/shard_map/all_gather | solution.py:66
  95.3 52.4 %all-reduce.5.cloned.1.call-done = f32[256,256]{0,1:T(8,128)} async-done(((f32[256,256]{0,1:T(8,128)}), f32[256,256]{0,1:T(8,128)}) %all-reduce.5.cloned.1.call-update) | async-done | bytes 262160 | tf_op jit(solution)/shard_map/psum | solution.py:121
  151.2 1.5 collective-permute-start.11
  152.9 2.4 collective-permute-start.12
  155.9 2.4 collective-permute-start.14
  159.4 1.7 collective-permute-done.13
  162.4 128.9 %all-reduce.7.cloned.1.call-done = (f32[256,128]{1,0:T(8,128)}, f32[256,256]{0,1:T(8,128)}) async-done(((f32[256,128]{1,0:T(8,128)}, f32[256,256]{0,1:T(8,128)}), (f32[256,128]{1,0:T(8,128)}, f32[256,256]{0,1:T(8,128)})) %all-reduce.7.cloned.1.call-update) | async-done | bytes 393232 | tf_op jit(solution)/shard_map/psum | solution.py:138
  291.3 1.7 multiply_add_fusion
  293.2 11.7 %cholesky.49 = f32[128,128]{1,0:T(8,128)S(1)} custom-call(f32[128,128]{1,0:T(8,128)S(1)} %cholesky.115), custom_call_target="Cholesky" | custom-call | tf_op jit(solution)/shard_map/jit(cholesky)/cholesky | solution.py:141
  304.9 9.8 %custom-call.18 = f32[1,128,128]{1,2,0:T(8,128)S(1)} custom-call(f32[1,128,128]{2,1,0:T(8,128)S(1)} %get-tuple-element.29), custom_call_target="InvertDiagBlocksLowerTriangular" | custom-call | tf_op jit(solution)/shard_map/jit(cholesky)/cholesky | solution.py:141
  315.2 11.7 %cholesky.103 = f32[128,128]{1,0:T(8,128)S(1)} custom-call(f32[128,128]{1,0:T(8,128)S(1)} %convolution_subtract_fusion.2), custom_call_target="Cholesky" | custom-call | tf_op jit(solution)/shard_map/jit(cholesky)/cholesky | solution.py:141
  329.4 4.4 %while.1 = (s32[]{:T(128)}, f32[256,256]{0,1:T(8,128)S(1)}, s32[2,2]{1,0:T(2,128)S(1)}, f32[2,128,128]{2,1,0:T(8,128)S(1)}, s32[]{:T(128)}) while((s32[]{:T(128)}, f32[256,256]{0,1:T(8,128)S(1)}, s32[2,2]{1,0:T(2,128)S(1)}, f32[2,128,128]{2,1,0:T(8,128)S(1)}, s32[]{:T(128)}) %tuple.27), condition=%wide.while_cond, body=%wide.while_body.sunk | while | flops 2 | bytes 393321 | solution.py:142
  330.1 1.4 dynamic-slice.7
  332.2 1.4 dynamic-slice.7
  333.7 19.7 %custom-call.19 = f32[2,128,128]{1,2,0:T(8,128)S(1)} custom-call(f32[2,128,128]{2,1,0:T(8,128)S(1)} %get-tuple-element.9), custom_call_target="InvertDiagBlocksLowerTriangular" | custom-call | tf_op jit(solution)/shard_map/jit(_cho_solve)/triangular_solve | solution.py:142
  (123 shorter events, 23.5 us)
Async XLA Ops:
  8.0 139.7 %all-reduce.5.cloned.1.call-start = ((), (), s32[]{:S(2)}) async-start(), calls=%async_computation.2 | async-start | bytes 524288 | tf_op jit(solution)/shard_map/psum | solution.py:121
  8.0 55.0 %collective-permute-start = (f32[64,256]{1,0:T(8,128)}, f32[64,256]{1,0:T(8,128)S(1)}, u32[]{:S(2)}, u32[]{:S(2)}) collective-permute-start(f32[64,256]{1,0:T(8,128)} %param.5), channel_id=1, source_target_pairs={{2,0},{4,2},{6,4},{8,6},{10,8},{12,10},{14,12},{16,14},{18,16},{20... | collective-permute-start | bytes 196616 | tf_op jit(solution)/shard_map/ppermute | solution.py:14
  13.6 54.8 %collective-permute-start.2 = (f32[64,256]{1,0:T(8,128)}, f32[64,256]{1,0:T(8,128)S(1)}, u32[]{:S(2)}, u32[]{:S(2)}) collective-permute-start(f32[64,256]{1,0:T(8,128)} %param.5), channel_id=1, source_target_pairs={{4,0},{6,2},{8,4},{10,6},{12,8},{14,10},{16,12},{18,14},{20,16},{2... | collective-permute-start | bytes 196616 | tf_op jit(solution)/shard_map/ppermute | solution.py:14
  14.2 59.7 %collective-permute-start.4 = (f32[64,256]{1,0:T(8,128)}, f32[64,256]{1,0:T(8,128)S(1)}, u32[]{:S(2)}, u32[]{:S(2)}) collective-permute-start(f32[64,256]{1,0:T(8,128)} %param.5), channel_id=1, source_target_pairs={{6,0},{8,2},{10,4},{12,6},{14,8},{16,10},{18,12},{20,14},{22,16},{... | collective-permute-start | bytes 196616 | tf_op jit(solution)/shard_map/ppermute | solution.py:14
  14.4 22.7 %collective-permute-start.1 = (f32[64,128]{1,0:T(8,128)}, f32[64,128]{1,0:T(8,128)S(1)}, u32[]{:S(2)}, u32[]{:S(2)}) collective-permute-start(f32[64,128]{1,0:T(8,128)} %param.6), channel_id=1, source_target_pairs={{2,0},{4,2},{6,4},{8,6},{10,8},{12,10},{14,12},{16,14},{18,16},{20... | collective-permute-start | bytes 98312 | tf_op jit(solution)/shard_map/ppermute | solution.py:14
  15.8 15.9 %collective-permute-start.9 = (f32[64,128]{1,0:T(8,128)}, f32[64,128]{1,0:T(8,128)S(1)}, u32[]{:S(2)}, u32[]{:S(2)}) collective-permute-start(f32[64,128]{1,0:T(8,128)} %param.6), channel_id=1, source_target_pairs={{16,0},{18,2},{20,4},{22,6},{24,8},{26,10},{28,12},{30,14},{0,16},... | collective-permute-start | bytes 98312 | tf_op jit(solution)/shard_map/ppermute | solution.py:14
  15.8 0.7 copy-start.7
  19.2 0.8 copy-start
  19.2 129.9 %reduce-scatter.2.cloned.1.call-start = ((), (), s32[]{:S(2)}) async-start(), calls=%async_computation.1 | async-start | bytes 589824 | tf_op jit(solution)/shard_map/reduce_scatter | solution.py:111
  20.2 5.1 %copy-start.1 = (f32[64,128]{1,0:T(8,128)S(1)}, f32[64,128]{1,0:T(8,128)}, u32[]{:S(2)}) copy-start(f32[64,128]{1,0:T(8,128)} %param.6) | copy-start | bytes 98308
  31.7 13.2 %collective-permute-start.5 = (f32[64,128]{1,0:T(8,128)S(1)}, f32[64,128]{1,0:T(8,128)S(1)}, u32[]{:S(2)}, u32[]{:S(2)}) collective-permute-start(f32[64,128]{1,0:T(8,128)S(1)} %copy-done.1), channel_id=1, source_target_pairs={{6,0},{8,2},{10,4},{12,6},{14,8},{16,10},{18,12},{20,14},{22,16},{... | collective-permute-start | bytes 98312 | tf_op jit(solution)/shard_map/ppermute | solution.py:14
  37.1 13.8 %collective-permute-start.7 = (f32[64,128]{1,0:T(8,128)S(1)}, f32[64,128]{1,0:T(8,128)S(1)}, u32[]{:S(2)}, u32[]{:S(2)}) collective-permute-start(f32[64,128]{1,0:T(8,128)S(1)} %copy-done.1), channel_id=1, source_target_pairs={{8,0},{10,2},{12,4},{14,6},{16,8},{18,10},{20,12},{22,14},{24,16},... | collective-permute-start | bytes 98312 | tf_op jit(solution)/shard_map/ppermute | solution.py:14
  44.9 10.7 %collective-permute-start.3 = (f32[64,128]{1,0:T(8,128)S(1)}, f32[64,128]{1,0:T(8,128)S(1)}, u32[]{:S(2)}, u32[]{:S(2)}) collective-permute-start(f32[64,128]{1,0:T(8,128)S(1)} %copy-done.1), channel_id=1, source_target_pairs={{4,0},{6,2},{8,4},{10,6},{12,8},{14,10},{16,12},{18,14},{20,16},{2... | collective-permute-start | bytes 98312 | tf_op jit(solution)/shard_map/ppermute | solution.py:14
  50.9 34.3 %collective-permute-start.6 = (f32[64,256]{1,0:T(8,128)S(1)}, f32[64,256]{1,0:T(8,128)S(1)}, u32[]{:S(2)}, u32[]{:S(2)}) collective-permute-start(f32[64,256]{1,0:T(8,128)S(1)} %copy-done), channel_id=1, source_target_pairs={{8,0},{10,2},{12,4},{14,6},{16,8},{18,10},{20,12},{22,14},{24,16},... | collective-permute-start | bytes 196616 | tf_op jit(solution)/shard_map/ppermute | solution.py:14
  55.5 24.4 %collective-permute-start.8 = (f32[64,256]{1,0:T(8,128)S(1)}, f32[64,256]{1,0:T(8,128)S(1)}, u32[]{:S(2)}, u32[]{:S(2)}) collective-permute-start(f32[64,256]{1,0:T(8,128)S(1)} %copy-done), channel_id=1, source_target_pairs={{16,0},{18,2},{20,4},{22,6},{24,8},{26,10},{28,12},{30,14},{0,16},... | collective-permute-start | bytes 196616 | tf_op jit(solution)/shard_map/ppermute | solution.py:14
  93.9 0.7 copy-start.3
  94.6 196.6 %all-reduce.7.cloned.1.call-start = ((), (), s32[]{:S(2)}) async-start(), calls=%async_computation.3 | async-start | bytes 786432 | tf_op jit(solution)/shard_map/psum | solution.py:138
  147.7 1.1 copy-start.2
  149.1 3.6 copy-start.5
  150.2 9.2 %collective-permute-start.10 = (f32[64,128]{1,0:T(8,128)S(1)}, f32[64,128]{1,0:T(8,128)S(1)}, u32[]{:S(2)}, u32[]{:S(2)}) collective-permute-start(f32[64,128]{1,0:T(8,128)S(1)} %convolution_add_fusion.3), channel_id=1, source_target_pairs={{30,0},{0,2},{2,4},{4,6},{6,8},{8,10},{10,12},{12,14},{14,16},{16,... | collective-permute-start | bytes 98312 | tf_op jit(solution)/shard_map/ppermute | solution.py:14
  151.2 8.2 %collective-permute-start.11 = (f32[64,128]{1,0:T(8,128)S(1)}, f32[64,128]{1,0:T(8,128)S(1)}, u32[]{:S(2)}, u32[]{:S(2)}) collective-permute-start(f32[64,128]{1,0:T(8,128)S(1)} %convolution_add_fusion.2), channel_id=1, source_target_pairs={{28,0},{30,2},{0,4},{2,6},{4,8},{6,10},{8,12},{10,14},{12,16},{14,... | collective-permute-start | bytes 98312 | tf_op jit(solution)/shard_map/ppermute | solution.py:14
  152.9 6.5 %collective-permute-start.12 = (f32[64,128]{1,0:T(8,128)S(1)}, f32[64,128]{1,0:T(8,128)S(1)}, u32[]{:S(2)}, u32[]{:S(2)}) collective-permute-start(f32[64,128]{1,0:T(8,128)S(1)} %convolution_add_fusion.1), channel_id=1, source_target_pairs={{26,0},{28,2},{30,4},{0,6},{2,8},{4,10},{6,12},{8,14},{10,16},{12,... | collective-permute-start | bytes 98312 | tf_op jit(solution)/shard_map/ppermute | solution.py:14
  155.3 5.7 %collective-permute-start.13 = (f32[64,128]{1,0:T(8,128)S(1)}, f32[64,128]{1,0:T(8,128)S(1)}, u32[]{:S(2)}, u32[]{:S(2)}) collective-permute-start(f32[64,128]{1,0:T(8,128)S(1)} %get-tuple-element.26), channel_id=1, source_target_pairs={{24,0},{26,2},{28,4},{30,6},{0,8},{2,10},{4,12},{6,14},{8,16},{10,... | collective-permute-start | bytes 98312 | tf_op jit(solution)/shard_map/ppermute | solution.py:14
  155.9 5.2 %collective-permute-start.14 = (f32[64,128]{1,0:T(8,128)S(1)}, f32[64,128]{1,0:T(8,128)S(1)}, u32[]{:S(2)}, u32[]{:S(2)}) collective-permute-start(f32[64,128]{1,0:T(8,128)S(1)} %get-tuple-element.27), channel_id=1, source_target_pairs={{16,0},{18,2},{20,4},{22,6},{24,8},{26,10},{28,12},{30,14},{0,16},... | collective-permute-start | bytes 98312 | tf_op jit(solution)/shard_map/ppermute | solution.py:14
  161.3 193.7 %copy-start.4 = (f32[64,128]{1,0:T(8,128)}, f32[64,128]{1,0:T(8,128)S(1)}, u32[]{:S(2)}) copy-start(f32[64,128]{1,0:T(8,128)S(1)} %fusion.31) | copy-start | bytes 98308
  329.4 24.0 %copy-start.6 = (f32[256,128]{1,0:T(8,128)S(1)}, f32[256,128]{1,0:T(8,128)}, u32[]{:S(2)}) copy-start(f32[256,128]{1,0:T(8,128)} %get-tuple-element.22) | copy-start | bytes 393220
Sparse Core Ops, SparseCore 0:
  19.4 128.3 all-reduce.4
  162.5 128.7 all-reduce.6
Sparse Core Ops, SparseCore 1:
  94.7 10.7 reduce-scatter.1
where the time goes:
time: 364 us; the launch traced here: 363 us
  waiting for transfers between devices  183 us (50%)
  blocking collectives  57.9 us (16%)
  other arithmetic  56.6 us (16%)
  starting transfers between devices  23.3 us (6%)
  between operations  18.6 us (5%)
  matrix products  14.9 us (4%)
  local copies, waits for them, and re-layouts  8.57 us (2%)
    psum x1, waiting for transfers between devices, per_device(): gram_sum, projected = lax.psum((gram_part, projected_part), ('blk', 'row'))  129 us
    psum x1, waiting for transfers between devices, per_device(): pivot_feats = lax.psum(picked, ('blk', 'row'))  52.4 us
    another operation x6, other arithmetic, per_device(): factor = jnp.linalg.cholesky(gram)  34 us
    all_gather x6, blocking collectives, member_sweep(): arrived_feats = lax.all_gather(fetched[upper][0], 'row', axis=0, tiled=True)  30.5 us
    all_gather x6, blocking collectives, member_sweep(): lax.all_gather(fetched[upper][1], 'row', axis=0, tiled=True)  27.4 us
    ppermute x15, starting transfers between devices, shifted(): return lax.ppermute(block, axis, route)  23.2 us
    another operation x3, other arithmetic, per_device(): coefficients = jax.scipy.linalg.cho_solve((factor, True), projected)  19.7 us
  transfers between devices with their start and end apart: 18, of which 3 were waited for; matrix products, arithmetic and copies ran while one was open for 4% of the time, Pallas kernels for 0%

commit v1 on v0

--- a/solution.py
+++ b/solution.py
@@ -118,7 +118,7 @@
     offsets = pivots - flat_index * local_rows
     inside = (offsets >= 0) & (offsets < local_rows)
     picked = jnp.where(inside[:, None], features[jnp.clip(offsets, 0, local_rows - 1)], 0.0)
-    pivot_feats = lax.psum(picked, ("blk", "row"))
+    pivot_feats = jnp.sum(lax.all_gather(picked, ("blk", "row")), axis=0)
     pivot_norms = jnp.sum(pivot_feats * pivot_feats, axis=1)
     cross = amplitude * kernel_tile(features, own_norms, pivot_feats, pivot_norms)
     gram_part = lax.dot_general(

time: 364 us -> 348 us (0.956)
  waiting for transfers between devices: 183 us -> 152 us
  matrix products: 14.9 us -> 24.3 us
  other arithmetic: 56.6 us -> 62.1 us
    psum x1 -> x0, waiting for transfers between devices: 52.4 us -> none  [per_device(): pivot_feats = lax.psum(picked, ('blk', 'row'))]
    all_gather x0 -> x1, waiting for transfers between devices: none -> 19.3 us  [per_device(): pivot_feats = jnp.sum(lax.all_gather(picked, ('blk', 'row')), axis=0)]
    reduce_sum x0 -> x1, other arithmetic: none -> 3.93 us  [per_device(): pivot_feats = jnp.sum(lax.all_gather(picked, ('blk', 'row')), axis=0)]
  transfers between devices with their start and end apart: 18 -> 18, of which waited for: 3 -> 5; matrix products, arithmetic and copies ran while one was open for 4% -> 6% of each run, Pallas kernels for 0% -> 0%
where the time goes in v1:
time: 348 us; the launch traced here: 347 us
  waiting for transfers between devices  152 us (44%)
  other arithmetic  62.1 us (18%)
  blocking collectives  60.7 us (17%)
  matrix products  24.3 us (7%)
  starting transfers between devices  20.9 us (6%)
  between operations  18.7 us (5%)
  local copies, waits for them, and re-layouts  8.01 us (2%)
    psum x1, waiting for transfers between devices, per_device(): gram_sum, projected = lax.psum((gram_part, projected_part), ('blk', 'row'))  128 us
    another operation x6, other arithmetic, per_device(): factor = jnp.linalg.cholesky(gram)  34.2 us
    all_gather x6, blocking collectives, member_sweep(): arrived_feats = lax.all_gather(fetched[upper][0], 'row', axis=0, tiled=True)  30.7 us
    all_gather x6, blocking collectives, member_sweep(): lax.all_gather(fetched[upper][1], 'row', axis=0, tiled=True)  30 us
    ppermute x15, starting transfers between devices, shifted(): return lax.ppermute(block, axis, route)  20.8 us
    another operation x3, other arithmetic, per_device(): coefficients = jax.scipy.linalg.cho_solve((factor, True), projected)  19.7 us
    all_gather x1, waiting for transfers between devices, per_device(): pivot_feats = jnp.sum(lax.all_gather(picked, ('blk', 'row')), axis=0)  19.3 us
    dot_general x11, matrix products, kernel_tile(): lax.dot_general(row_feats, col_feats, (((1,), (1,)), ((), ())), precision...  7.9 us
  transfers between devices with their start and end apart: 18, of which 5 were waited for; matrix products, arithmetic and copies ran while one was open for 6% of the time, Pallas kernels for 0%

profile of v1, /device:TPU:0, one launch (start us, length us, event | category | flops | bytes accessed | tf_op | source)
XLA Modules:
  0.0 346.6 jit_solution(14330757230509133230)
XLA Ops:
  8.1 5.5 %collective-permute-start = (f32[64,256]{1,0:T(8,128)}, f32[64,256]{1,0:T(8,128)S(1)}, u32[]{:S(2)}, u32[]{:S(2)}) collective-permute-start(f32[64,256]{1,0:T(8,128)} %param.5), channel_id=1, source_target_pairs={{2,0},{4,2},{6,4},{8,6},{10,8},{12,10},{14,12},{16,14},{18,16},{20... | collective-permute-start | bytes 196616 | tf_op jit(solution)/shard_map/ppermute | solution.py:14
  14.9 2.6 collective-permute-start.8
  18.5 2.0 collective-permute-start.3
  20.5 5.0 %all_gather.42 = f32[128,256]{1,0:T(8,128)S(1)} all-gather(f32[64,256]{1,0:T(8,128)S(1)} %collective-permute-done), channel_id=1, replica_groups=mesh['blk'=16,'row'=2] {'row'}, dimensions={0}, use_global_device_ids=true | all-gather | bytes 196608 | tf_op jit(solution)/shard_map/all_gather | solution.py:66
  25.7 5.1 %all_gather.44 = f32[128,256]{1,0:T(8,128)S(1)} all-gather(f32[64,256]{1,0:T(8,128)S(1)} %collective-permute-done.2), channel_id=1, replica_groups=mesh['blk'=16,'row'=2] {'row'}, dimensions={0}, use_global_device_ids=true | all-gather | bytes 196608 | tf_op jit(solution)/shard_map/all_gather | solution.py:66
  33.3 5.5 %all_gather.46 = f32[128,256]{1,0:T(8,128)S(1)} all-gather(f32[64,256]{1,0:T(8,128)S(1)} %collective-permute-done.4), channel_id=1, replica_groups=mesh['blk'=16,'row'=2] {'row'}, dimensions={0}, use_global_device_ids=true | all-gather | bytes 196608 | tf_op jit(solution)/shard_map/all_gather | solution.py:66
  39.0 1.1 exponential_multiply_fusion.4
  40.1 4.9 %all_gather.48 = f32[128,256]{1,0:T(8,128)S(1)} all-gather(f32[64,256]{1,0:T(8,128)S(1)} %collective-permute-done.6), channel_id=1, replica_groups=mesh['blk'=16,'row'=2] {'row'}, dimensions={0}, use_global_device_ids=true | all-gather | bytes 196608 | tf_op jit(solution)/shard_map/all_gather | solution.py:66
  46.3 4.9 %all_gather.50 = f32[128,256]{1,0:T(8,128)S(1)} all-gather(f32[64,256]{1,0:T(8,128)S(1)} %collective-permute-done.8), channel_id=1, replica_groups=mesh['blk'=16,'row'=2] {'row'}, dimensions={0}, use_global_device_ids=true | all-gather | bytes 196608 | tf_op jit(solution)/shard_map/all_gather | solution.py:66
  59.3 1.8 gather_fusion
  62.8 3.4 collective-permute-start.7
  67.5 5.6 %all_gather.41 = f32[128,128]{1,0:T(8,128)S(1)} all-gather(f32[64,128]{1,0:T(8,128)} %param.6), channel_id=1, replica_groups=mesh['blk'=16,'row'=2] {'row'}, dimensions={0}, use_global_device_ids=true | all-gather | bytes 98304 | tf_op jit(solution)/shard_map/all_gather | solution.py:67
  73.0 5.1 %all_gather.40 = f32[128,256]{1,0:T(8,128)S(1)} all-gather(f32[64,256]{1,0:T(8,128)} %param.5), channel_id=1, replica_groups=mesh['blk'=16,'row'=2] {'row'}, dimensions={0}, use_global_device_ids=true | all-gather | bytes 196608 | tf_op jit(solution)/shard_map/all_gather | solution.py:66
  78.8 4.6 %all_gather.43 = f32[128,128]{1,0:T(8,128)S(1)} all-gather(f32[64,128]{1,0:T(8,128)S(1)} %collective-permute-done.1), channel_id=1, replica_groups=mesh['blk'=16,'row'=2] {'row'}, dimensions={0}, use_global_device_ids=true | all-gather | bytes 98304 | tf_op jit(solution)/shard_map/all_gather | solution.py:67
  83.4 4.6 %all_gather.47 = f32[128,128]{1,0:T(8,128)S(1)} all-gather(f32[64,128]{1,0:T(8,128)S(1)} %collective-permute-done.5), channel_id=1, replica_groups=mesh['blk'=16,'row'=2] {'row'}, dimensions={0}, use_global_device_ids=true | all-gather | bytes 98304 | tf_op jit(solution)/shard_map/all_gather | solution.py:67
  87.9 5.9 %all_gather.45 = f32[128,128]{1,0:T(8,128)S(1)} all-gather(f32[64,128]{1,0:T(8,128)S(1)} %collective-permute-done.3), channel_id=1, replica_groups=mesh['blk'=16,'row'=2] {'row'}, dimensions={0}, use_global_device_ids=true | all-gather | bytes 98304 | tf_op jit(solution)/shard_map/all_gather | solution.py:67
  93.8 4.7 %all_gather.51 = f32[128,128]{1,0:T(8,128)S(1)} all-gather(f32[64,128]{1,0:T(8,128)S(1)} %collective-permute-done.9), channel_id=1, replica_groups=mesh['blk'=16,'row'=2] {'row'}, dimensions={0}, use_global_device_ids=true | all-gather | bytes 98304 | tf_op jit(solution)/shard_map/all_gather | solution.py:67
  98.6 4.6 %all_gather.49 = f32[128,128]{1,0:T(8,128)S(1)} all-gather(f32[64,128]{1,0:T(8,128)S(1)} %collective-permute-done.7), channel_id=1, replica_groups=mesh['blk'=16,'row'=2] {'row'}, dimensions={0}, use_global_device_ids=true | all-gather | bytes 98304 | tf_op jit(solution)/shard_map/all_gather | solution.py:67
  109.2 4.3 %collective-permute-start.14 = (f32[64,128]{1,0:T(8,128)S(1)}, f32[64,128]{1,0:T(8,128)S(1)}, u32[]{:S(2)}, u32[]{:S(2)}) collective-permute-start(f32[64,128]{1,0:T(8,128)S(1)} %get-tuple-element.35), channel_id=1, source_target_pairs={{16,0},{18,2},{20,4},{22,6},{24,8},{26,10},{28,12},{30,14},{0,16},... | collective-permute-start | bytes 98312 | tf_op jit(solution)/shard_map/ppermute | solution.py:14
  114.0 1.9 collective-permute-done.13
  115.9 2.5 collective-permute-done.14
  119.4 19.3 %all-gather.2.cloned.1.call-done = f32[32,256,256]{2,1,0:T(8,128)} async-done(((f32[1,256,256]{2,1,0:T(8,128)}), f32[32,256,256]{2,1,0:T(8,128)}) %all-gather.2.cloned.1.call-update) | async-done | bytes 8388624 | tf_op jit(solution)/shard_map/all_gather | solution.py:121
  138.7 3.9 %reduce_sum.122 = f32[256,256]{1,0:T(8,128)S(1)} reduce(f32[32,256,256]{2,1,0:T(8,128)} %all-gather.2.cloned.1.call-done, f32[]{:T(128)} %constant.123.clone.1), dimensions={0}, to_apply=%region_11.0 | reduce | flops 2031616 | bytes 8650756 | tf_op jit(solution)/shard_map/reduce_sum | solution.py:121
  145.3 127.8 %all-reduce.4.cloned.1.call-done = (f32[256,128]{1,0:T(8,128)}, f32[256,256]{0,1:T(8,128)}) async-done(((f32[256,128]{1,0:T(8,128)}, f32[256,256]{0,1:T(8,128)}), (f32[256,128]{1,0:T(8,128)}, f32[256,256]{0,1:T(8,128)})) %all-reduce.4.cloned.1.call-update) | async-done | bytes 393232 | tf_op jit(solution)/shard_map/psum | solution.py:138
  273.1 1.5 multiply_add_fusion
  274.8 11.7 %cholesky.49 = f32[128,128]{1,0:T(8,128)S(1)} custom-call(f32[128,128]{1,0:T(8,128)S(1)} %cholesky.115), custom_call_target="Cholesky" | custom-call | tf_op jit(solution)/shard_map/jit(cholesky)/cholesky | solution.py:141
  286.6 9.8 %custom-call.18 = f32[1,128,128]{1,2,0:T(8,128)S(1)} custom-call(f32[1,128,128]{2,1,0:T(8,128)S(1)} %get-tuple-element.37), custom_call_target="InvertDiagBlocksLowerTriangular" | custom-call | tf_op jit(solution)/shard_map/jit(cholesky)/cholesky | solution.py:141
  296.9 11.9 %cholesky.103 = f32[128,128]{1,0:T(8,128)S(1)} custom-call(f32[128,128]{1,0:T(8,128)S(1)} %convolution_subtract_fusion.2), custom_call_target="Cholesky" | custom-call | tf_op jit(solution)/shard_map/jit(cholesky)/cholesky | solution.py:141
  311.2 4.2 %while.1 = (s32[]{:T(128)}, f32[256,256]{0,1:T(8,128)S(1)}, s32[2,2]{1,0:T(2,128)S(1)}, f32[2,128,128]{2,1,0:T(8,128)S(1)}, s32[]{:T(128)}) while((s32[]{:T(128)}, f32[256,256]{0,1:T(8,128)S(1)}, s32[2,2]{1,0:T(2,128)S(1)}, f32[2,128,128]{2,1,0:T(8,128)S(1)}, s32[]{:T(128)}) %tuple.29), condition=%wide.while_cond, body=%wide.while_body.sunk | while | flops 2 | bytes 393321 | solution.py:142
  311.8 1.4 dynamic-slice.7
  313.9 1.4 dynamic-slice.7
  315.4 19.7 %custom-call.19 = f32[2,128,128]{1,2,0:T(8,128)S(1)} custom-call(f32[2,128,128]{2,1,0:T(8,128)S(1)} %get-tuple-element.9), custom_call_target="InvertDiagBlocksLowerTriangular" | custom-call | tf_op jit(solution)/shard_map/jit(_cho_solve)/triangular_solve | solution.py:142
  (115 shorter events, 33.7 us)
Async XLA Ops:
  8.0 70.3 %copy-start = (f32[64,256]{1,0:T(8,128)S(1)}, f32[64,256]{1,0:T(8,128)}, u32[]{:S(2)}) copy-start(f32[64,256]{1,0:T(8,128)} %param.5) | copy-start | bytes 196612
  8.0 110.4 %copy-start.1 = (f32[64,128]{1,0:T(8,128)S(1)}, f32[64,128]{1,0:T(8,128)}, u32[]{:S(2)}) copy-start(f32[64,128]{1,0:T(8,128)} %param.6) | copy-start | bytes 98308
  8.0 96.1 %reduce-scatter.2.cloned.1.call-start = ((), (), s32[]{:S(2)}) async-start(), calls=%async_computation.1 | async-start | bytes 589824 | tf_op jit(solution)/shard_map/reduce_scatter | solution.py:111
  8.1 10.4 %collective-permute-start = (f32[64,256]{1,0:T(8,128)}, f32[64,256]{1,0:T(8,128)S(1)}, u32[]{:S(2)}, u32[]{:S(2)}) collective-permute-start(f32[64,256]{1,0:T(8,128)} %param.5), channel_id=1, source_target_pairs={{2,0},{4,2},{6,4},{8,6},{10,8},{12,10},{14,12},{16,14},{18,16},{20... | collective-permute-start | bytes 196616 | tf_op jit(solution)/shard_map/ppermute | solution.py:14
  13.6 12.1 %collective-permute-start.2 = (f32[64,256]{1,0:T(8,128)}, f32[64,256]{1,0:T(8,128)S(1)}, u32[]{:S(2)}, u32[]{:S(2)}) collective-permute-start(f32[64,256]{1,0:T(8,128)} %param.5), channel_id=1, source_target_pairs={{4,0},{6,2},{8,4},{10,6},{12,8},{14,10},{16,12},{18,14},{20,16},{2... | collective-permute-start | bytes 196616 | tf_op jit(solution)/shard_map/ppermute | solution.py:14
  14.2 19.1 %collective-permute-start.4 = (f32[64,256]{1,0:T(8,128)}, f32[64,256]{1,0:T(8,128)S(1)}, u32[]{:S(2)}, u32[]{:S(2)}) collective-permute-start(f32[64,256]{1,0:T(8,128)} %param.5), channel_id=1, source_target_pairs={{6,0},{8,2},{10,4},{12,6},{14,8},{16,10},{18,12},{20,14},{22,16},{... | collective-permute-start | bytes 196616 | tf_op jit(solution)/shard_map/ppermute | solution.py:14
  14.4 25.7 %collective-permute-start.6 = (f32[64,256]{1,0:T(8,128)}, f32[64,256]{1,0:T(8,128)S(1)}, u32[]{:S(2)}, u32[]{:S(2)}) collective-permute-start(f32[64,256]{1,0:T(8,128)} %param.5), channel_id=1, source_target_pairs={{8,0},{10,2},{12,4},{14,6},{16,8},{18,10},{20,12},{22,14},{24,16},... | collective-permute-start | bytes 196616 | tf_op jit(solution)/shard_map/ppermute | solution.py:14
  14.9 31.4 %collective-permute-start.8 = (f32[64,256]{1,0:T(8,128)}, f32[64,256]{1,0:T(8,128)S(1)}, u32[]{:S(2)}, u32[]{:S(2)}) collective-permute-start(f32[64,256]{1,0:T(8,128)} %param.5), channel_id=1, source_target_pairs={{16,0},{18,2},{20,4},{22,6},{24,8},{26,10},{28,12},{30,14},{0,16},... | collective-permute-start | bytes 196616 | tf_op jit(solution)/shard_map/ppermute | solution.py:14
  18.5 38.4 %collective-permute-start.3 = (f32[64,128]{1,0:T(8,128)}, f32[64,128]{1,0:T(8,128)S(1)}, u32[]{:S(2)}, u32[]{:S(2)}) collective-permute-start(f32[64,128]{1,0:T(8,128)} %param.6), channel_id=1, source_target_pairs={{4,0},{6,2},{8,4},{10,6},{12,8},{14,10},{16,12},{18,14},{20,16},{2... | collective-permute-start | bytes 98312 | tf_op jit(solution)/shard_map/ppermute | solution.py:14
  25.7 31.5 %collective-permute-start.1 = (f32[64,128]{1,0:T(8,128)}, f32[64,128]{1,0:T(8,128)S(1)}, u32[]{:S(2)}, u32[]{:S(2)}) collective-permute-start(f32[64,128]{1,0:T(8,128)} %param.6), channel_id=1, source_target_pairs={{2,0},{4,2},{6,4},{8,6},{10,8},{12,10},{14,12},{16,14},{18,16},{20... | collective-permute-start | bytes 98312 | tf_op jit(solution)/shard_map/ppermute | solution.py:14
  33.3 24.2 %collective-permute-start.5 = (f32[64,128]{1,0:T(8,128)}, f32[64,128]{1,0:T(8,128)S(1)}, u32[]{:S(2)}, u32[]{:S(2)}) collective-permute-start(f32[64,128]{1,0:T(8,128)} %param.6), channel_id=1, source_target_pairs={{6,0},{8,2},{10,4},{12,6},{14,8},{16,10},{18,12},{20,14},{22,16},{... | collective-permute-start | bytes 98312 | tf_op jit(solution)/shard_map/ppermute | solution.py:14
  57.8 0.8 copy-start.2
  58.6 80.1 %all-gather.2.cloned.1.call-start = ((), (), s32[]{:S(2)}) async-start(), calls=%async_computation.2 | async-start | bytes 8650752 | tf_op jit(solution)/shard_map/all_gather | solution.py:121
  62.7 210.4 %all-reduce.4.cloned.1.call-start = ((), (), s32[]{:S(2)}) async-start(), calls=%async_computation.3 | async-start | bytes 786432 | tf_op jit(solution)/shard_map/psum | solution.py:138
  62.7 31.1 %collective-permute-start.9 = (f32[64,128]{1,0:T(8,128)}, f32[64,128]{1,0:T(8,128)S(1)}, u32[]{:S(2)}, u32[]{:S(2)}) collective-permute-start(f32[64,128]{1,0:T(8,128)} %param.6), channel_id=1, source_target_pairs={{16,0},{18,2},{20,4},{22,6},{24,8},{26,10},{28,12},{30,14},{0,16},... | collective-permute-start | bytes 98312 | tf_op jit(solution)/shard_map/ppermute | solution.py:14
  62.8 35.8 %collective-permute-start.7 = (f32[64,128]{1,0:T(8,128)}, f32[64,128]{1,0:T(8,128)S(1)}, u32[]{:S(2)}, u32[]{:S(2)}) collective-permute-start(f32[64,128]{1,0:T(8,128)} %param.6), channel_id=1, source_target_pairs={{8,0},{10,2},{12,4},{14,6},{16,8},{18,10},{20,12},{22,14},{24,16},... | collective-permute-start | bytes 98312 | tf_op jit(solution)/shard_map/ppermute | solution.py:14
  105.1 8.6 %collective-permute-start.10 = (f32[64,128]{1,0:T(8,128)S(1)}, f32[64,128]{1,0:T(8,128)S(1)}, u32[]{:S(2)}, u32[]{:S(2)}) collective-permute-start(f32[64,128]{1,0:T(8,128)S(1)} %convolution_add_fusion.3), channel_id=1, source_target_pairs={{30,0},{0,2},{2,4},{4,6},{6,8},{8,10},{10,12},{12,14},{14,16},{16,... | collective-permute-start | bytes 98312 | tf_op jit(solution)/shard_map/ppermute | solution.py:14
  106.1 7.6 %collective-permute-start.11 = (f32[64,128]{1,0:T(8,128)S(1)}, f32[64,128]{1,0:T(8,128)S(1)}, u32[]{:S(2)}, u32[]{:S(2)}) collective-permute-start(f32[64,128]{1,0:T(8,128)S(1)} %convolution_add_fusion.2), channel_id=1, source_target_pairs={{28,0},{30,2},{0,4},{2,6},{4,8},{6,10},{8,12},{10,14},{12,16},{14,... | collective-permute-start | bytes 98312 | tf_op jit(solution)/shard_map/ppermute | solution.py:14
  107.1 6.9 %collective-permute-start.12 = (f32[64,128]{1,0:T(8,128)S(1)}, f32[64,128]{1,0:T(8,128)S(1)}, u32[]{:S(2)}, u32[]{:S(2)}) collective-permute-start(f32[64,128]{1,0:T(8,128)S(1)} %convolution_add_fusion.1), channel_id=1, source_target_pairs={{26,0},{28,2},{30,4},{0,6},{2,8},{4,10},{6,12},{8,14},{10,16},{12,... | collective-permute-start | bytes 98312 | tf_op jit(solution)/shard_map/ppermute | solution.py:14
  108.4 7.5 %collective-permute-start.13 = (f32[64,128]{1,0:T(8,128)S(1)}, f32[64,128]{1,0:T(8,128)S(1)}, u32[]{:S(2)}, u32[]{:S(2)}) collective-permute-start(f32[64,128]{1,0:T(8,128)S(1)} %get-tuple-element.34), channel_id=1, source_target_pairs={{24,0},{26,2},{28,4},{30,6},{0,8},{2,10},{4,12},{6,14},{8,16},{10,... | collective-permute-start | bytes 98312 | tf_op jit(solution)/shard_map/ppermute | solution.py:14
  109.2 9.2 %collective-permute-start.14 = (f32[64,128]{1,0:T(8,128)S(1)}, f32[64,128]{1,0:T(8,128)S(1)}, u32[]{:S(2)}, u32[]{:S(2)}) collective-permute-start(f32[64,128]{1,0:T(8,128)S(1)} %get-tuple-element.35), channel_id=1, source_target_pairs={{16,0},{18,2},{20,4},{22,6},{24,8},{26,10},{28,12},{30,14},{0,16},... | collective-permute-start | bytes 98312 | tf_op jit(solution)/shard_map/ppermute | solution.py:14
  119.4 218.9 %copy-start.3 = (f32[64,128]{1,0:T(8,128)}, f32[64,128]{1,0:T(8,128)S(1)}, u32[]{:S(2)}) copy-start(f32[64,128]{1,0:T(8,128)S(1)} %fusion.31) | copy-start | bytes 98308
Sparse Core Ops, SparseCore 0:
  58.7 11.2 reduce-scatter.1
Sparse Core Ops, SparseCore 1:
  62.7 75.9 all-gather.1
  145.4 127.7 all-reduce.3
